TPU v7x, 768 devices: a whole 4x8x12 slice. The times are simulated.
768 devices in a mesh: gx: 4 (over x), gy: 12 (over z), gz: 16 (over y, core).
Axes of the slice: x: 4, y: 8, z: 12, core: 2. Of those that a mesh axis runs over, the one named last changes fastest.
Arguments:
- conductivity: float32 [32, 96, 4096], P('gx', 'gy', 'gz'), may hold values from 0.1 to 10
- source: float32 [32, 96, 4096], P('gx', 'gy', 'gz'), may hold values from -5 to 5
Outputs:
- solution: float32 [32, 96, 4096], P('gx', 'gy', 'gz')
- residual: float32 [32, 96, 4096], P('gx', 'gy', 'gz')
All inputs are finite; a program needn't handle non-finite values.
Results may differ from a plain program's by a relative error of at most 0.0003.
Values sent between devices are 32-bit elements; how exact they have to be, the bound alone decides.
A program may use at most 64 MiB of HBM per device.

v0:
```python
import jax
import jax.numpy as jnp
from jax import lax
from jax.experimental import pallas as pl
from jax.experimental.pallas import tpu as pltpu
from jax.sharding import PartitionSpec as P

MESH = pl.DeviceIdType.MESH
F32 = jnp.float32
DEGREE = 4
COARSE_DEGREE = 8
UPPER = 2.0
FINE_LOW = 0.5
COARSE_LOW = 0.03
REACH = 5
SPAN = 2 * REACH + 1

P0, W0 = 5, 8
P1, W1 = 4, 8
P2, W2 = 2, 18
SIDES = (-1, 0, 1)
FLAT = [(i, j, 0) for i in SIDES for j in SIDES if (i, j) != (0, 0)]
STACK = [(i, j, k) for k in (-1, 1) for i in SIDES for j in SIDES]
AROUND = STACK + sorted(FLAT, key=lambda o: -abs(o[0]) - abs(o[1]))


def chebyshev_coefs(degree, lower):
    centre = (UPPER + lower) / 2.0
    half_width = (UPPER - lower) / 2.0
    ratio_term = centre / half_width
    rho_prev = 1.0 / ratio_term
    weights = []
    for _ in range(1, degree):
        rho_next = 1.0 / (2.0 * ratio_term - rho_prev)
        weights.append((rho_next * rho_prev, 2.0 * rho_next / half_width))
        rho_prev = rho_next
    return 1.0 / centre, weights


def rolled(values, shift):
    flat = values.reshape(-1, 128)
    return pltpu.roll(flat, shift % 128, 1).reshape(values.shape)


def lanes_of(shape):
    return lax.broadcasted_iota(jnp.int32, shape, len(shape) - 1)


def beside(values):
    up, down = rolled(values, 1), rolled(values, -1)
    tiles = values.shape[1]
    if tiles > 1:
        lane = lanes_of(values.shape)
        before = jnp.concatenate([up[:, tiles - 1 :], up[:, : tiles - 1]], axis=1)
        after = jnp.concatenate([down[:, 1:], down[:, :1]], axis=1)
        up = jnp.where(lane == 0, before, up)
        down = jnp.where(lane == 127, after, down)
    return up + down


def stencil_sum(ref, first, count, row, rows):
    planes = pl.ds(first - 1, count + 2)
    centre = ref[planes, :, pl.ds(row, rows), :]
    side = ref[planes, :, pl.ds(row - 1, rows), :] + ref[planes, :, pl.ds(row + 1, rows), :]
    corner = 3.0 * centre + side
    face = 14.0 * centre + 3.0 * side
    outer = face[1:-1] + corner[:-2] + corner[2:]
    middle = 14.0 * side[1:-1] + face[:-2] + face[2:]
    return middle + beside(outer)


def chunks(first, last, size):
    return [(at, min(size, last - at)) for at in range(first, last, size)]


def apply(level, source, r_in, r_out, planes, row, rows, coefs, target=None, tiles=None, keep=None, size=2):
    kappa, diagonal, inverse = level
    v_ref, w_ref = source
    for first, count in chunks(planes[0], planes[1], size):
        at = (pl.ds(first, count), slice(None), pl.ds(row, rows), slice(None))
        v = v_ref[at]
        r = r_in(at) - diagonal[at] * v
        r = r + kappa[at] * stencil_sum(v_ref, first, count, row, rows)
        r = r + stencil_sum(w_ref, first, count, row, rows)
        if r_out is not None:
            r_out(first, count, r)
        if coefs is not None:
            new = (coefs[1] * inverse[at]) * r
            if coefs[0] is not None:
                new = new + coefs[0] * v
            target[0][at] = new
            if target[1] is not None:
                target[1][at] = kappa[at] * new


def pair_gather(values, index):
    return jnp.take_along_axis(values, index, axis=1)


def kernel(sizes, k_ref, b_ref, x_ref, r_ref, ext, edge_in, edge_out, redge_in, redge_out, rext,
           kap0, dia0, inv0, res0, va0, wa0, vb0, wb0, xs0,
           kin1, bin1, kap1, dia1, inv1, res1, va1, wa1, vb1, wb1, rex1, xex1, xs1,
           kap2, dia2, inv2, bin2, res2, va2, wa2, vb2, wb2, xs2, tmp, tmp2, send, recv):
    nx, ny, nz = sizes
    mx, my, mz = lax.axis_index("gx"), lax.axis_index("gy"), lax.axis_index("gz")
    used = [0]
    pending = []

    def inside(i, j, k):
        tests = []
        if i < 0:
            tests.append(mx + i >= 0)
        if i > 0:
            tests.append(mx + i < nx)
        if j < 0:
            tests.append(my + j >= 0)
        if j > 0:
            tests.append(my + j < ny)
        if k < 0:
            tests.append(mz + k >= 0)
        if k > 0:
            tests.append(mz + k < nz)
        ok = tests[0]
        for test in tests[1:]:
            ok = ok & test
        return ok

    def exchange(offsets, ends):
        base = used[0]
        used[0] += len(offsets)
        copies = []
        for n, (i, j, k) in enumerate(offsets):
            src, dst = ends(i, j, k)
            copy = pltpu.make_async_remote_copy(
                src_ref=src, dst_ref=dst, send_sem=send.at[base + n], recv_sem=recv.at[base + n],
                device_id=(mx + i, my + j, mz + k), device_id_type=MESH,
            )
            ok = inside(i, j, k)
            pl.when(ok)(copy.start)
            pending.append((ok, copy))
            copies.append((inside(-i, -j, -k), copy))

        def arrive():
            for ok, copy in copies:
                pl.when(ok)(copy.wait_recv)

        return arrive

    def plane_gather(ref):
        base = used[0]
        used[0] += nx * SPAN
        arrivals = []
        for j in sorted(range(-REACH, REACH + 1), key=lambda o: -abs(o)):
            if abs(j) >= ny:
                continue
            for gx in range(nx):
                ok = gx != mx if j == 0 else inside(0, j, 0)
                mine = (pl.ds(P2 + 2 * mx, 2), slice(None), pl.ds(W2, 2), slice(None))
                there = (pl.ds(P2 + 2 * mx, 2), slice(None), pl.ds(W2 - 2 * j, 2), slice(None))
                copy = pltpu.make_async_remote_copy(
                    src_ref=ref.at[mine], dst_ref=ref.at[there],
                    send_sem=send.at[base + gx * SPAN + j + REACH], recv_sem=recv.at[base + mx * SPAN + j + REACH],
                    device_id=(gx, my + j, mz), device_id_type=MESH,
                )
                pl.when(ok)(copy.start)
                pending.append((ok, copy))
                back = pltpu.make_async_remote_copy(
                    src_ref=ref.at[mine], dst_ref=ref.at[there],
                    send_sem=send.at[base + gx * SPAN + j + REACH], recv_sem=recv.at[base + gx * SPAN + j + REACH],
                    device_id=(gx, my, mz), device_id_type=MESH,
                )
                arrivals.append((gx != mx if j == 0 else inside(0, -j, 0), back))

        def arrive():
            for ok, copy in arrivals:
                pl.when(ok)(copy.wait_recv)

        return arrive

    def zero(ref):
        ref[...] = jnp.zeros(ref.shape, F32)

    def coarse_of(read, count, rows):
        for tile in range(2):
            for i in range(count):
                total = read(2 * i, 0, tile) + read(2 * i, 1, tile) + read(2 * i + 1, 0, tile) + read(2 * i + 1, 1, tile)
                tmp[tile, rows * i : rows * (i + 1), :] = 0.125 * total
        size = max(8, count * rows)
        lane = lanes_of((size, 128))
        pairs = [tmp[tile, 0:size, :] for tile in range(2)]
        pairs = [p + pltpu.roll(p, 127, 1) for p in pairs]
        index = (2 * lane) % 128
        out = jnp.where(lane < 64, pair_gather(pairs[0], index), pair_gather(pairs[1], index))
        tmp2[0:size, :] = out
        return [tmp2[rows * i : rows * (i + 1), :] for i in range(count)]

    def pack_edges(reads, out):
        for way, (tile, start) in enumerate(((1, 120), (0, 0))):
            packed = jnp.zeros((8, 128), F32)
            lane = lanes_of((8, 128))
            for a, read in enumerate(reads):
                for i in range(8):
                    at = 8 * i + 64 * a
                    part = pltpu.roll(read(i, tile), (at - start) % 128, 1)
                    packed = jnp.where((lane >= at) & (lane < at + 8), part, packed)
            out[way] = packed

    def edge_ends(src, dst):
        def ends(i, j, k):
            way, side = (0, 0) if k > 0 else (1, 1)
            return src.at[way], dst.at[side, 1 - i, pl.ds(8 * (1 - j), 8), :]

        return ends

    def unpack_edges(src, a, write):
        lane = lanes_of((24, 128))
        for p in range(2 * P0 + 8):
            group, i = (0, 3 + p) if p < P0 else ((1, p - P0) if p < P0 + 8 else (2, p - P0 - 8))
            at = 8 * i + 64 * a
            low = pltpu.roll(src[0, group], (120 - at) % 128, 1)
            high = pltpu.roll(src[1, group], -at % 128, 1)
            write(p, jnp.where(lane < 8, high, jnp.where(lane >= 120, low, 0.0)))

    def fine_slices(i, j):
        src_planes = {1: pl.ds(P0 + 3, 5), 0: pl.ds(P0, 8), -1: pl.ds(P0, 5)}[i]
        dst_planes = {1: pl.ds(0, 5), 0: pl.ds(P0, 8), -1: pl.ds(P0 + 8, 5)}[i]
        src_rows = {1: pl.ds(W0 + 3, 5), 0: pl.ds(W0, 8), -1: pl.ds(W0, 5)}[j]
        dst_rows = {1: pl.ds(W0 - 5, 5), 0: pl.ds(W0, 8), -1: pl.ds(W0 + 8, 5)}[j]
        return (src_planes, pl.ds(0, 2), src_rows), (dst_planes, pl.ds(0, 2), dst_rows)

    def coarse_slices(i, j):
        return (pl.ds(P1, 4), pl.ds(W1, 4)), (pl.ds(P1 - 4 * i, 4), pl.ds(W1 - 4 * j, 4))

    def level1_ends(ref):
        def ends(i, j, k):
            (sp, sr), (dp, dr) = coarse_slices(i, j)
            slot = {0: 0, -1: 1, 1: 2}[k]
            return ref.at[0, sp, sr, :], ref.at[slot, dp, dr, :]

        return ends

    def flat1_ends(ref):
        def ends(i, j, k):
            (sp, sr), (dp, dr) = coarse_slices(i, j)
            return ref.at[sp, :, sr, :], ref.at[dp, :, dr, :]

        return ends

    for ref in (ext, edge_in, kin1, kap2, bin2):
        zero(ref)
    for tile in range(2):
        cols = slice(128 * tile, 128 * tile + 128)
        ext[0, P0 : P0 + 8, tile, W0 : W0 + 8, :] = b_ref[:, :, cols]
        ext[1, P0 : P0 + 8, tile, W0 : W0 + 8, :] = k_ref[:, :, cols]

    barrier = pltpu.get_barrier_semaphore()

    def greet(ok, i, j, k):
        @pl.when(ok)
        def _():
            pl.semaphore_signal(barrier, inc=1, device_id=(i, j, k), device_id_type=MESH)

        return jnp.where(ok, 1, 0)

    count = 0
    for i, j, k in STACK:
        count = count + greet(inside(i, j, k), mx + i, my + j, mz + k)
    for j in range(-REACH, REACH + 1):
        if abs(j) < ny:
            for gx in range(nx):
                count = count + greet(gx != mx if j == 0 else inside(0, j, 0), gx, my + j, mz)

    for ref in (redge_in, rext, va0, wa0, vb0, wb0, bin1, dia1, va1, wa1, vb1, wb1, rex1, xex1, va2, wa2, vb2, wb2, xs2, tmp):
        zero(ref)
    pack_edges([lambda i, t: ext[0, P0 + i, t, W0 : W0 + 8, :], lambda i, t: ext[1, P0 + i, t, W0 : W0 + 8, :]], edge_out)
    own_k1 = coarse_of(lambda i, parity, t: ext[1, P0 + i, t, pl.ds(W0 + parity, 4, stride=2), :], 4, 4)
    for i, value in enumerate(own_k1):
        kin1[0, P1 + i, W1 : W1 + 4, :] = value

    pl.semaphore_wait(barrier, count)

    edges_arrive = exchange(STACK, edge_ends(edge_out, edge_in))

    def fine_ends(i, j, k):
        (sp, st, sr), (dp, dt, dr) = fine_slices(i, j)
        return ext.at[:, sp, st, sr, :], ext.at[:, dp, dt, dr, :]

    fine_arrive = exchange(sorted(FLAT, key=lambda o: -abs(o[0]) - abs(o[1])), fine_ends)
    k1_arrive = exchange(AROUND, level1_ends(kin1))
    edges_arrive()
    fine_arrive()

    def put(a):
        def write(p, value):
            ext[a, p, 2] = value

        return write

    unpack_edges(edge_in, 0, put(0))
    unpack_edges(edge_in, 1, put(1))
    for first, n in chunks(0, 18, 3):
        kap0[first : first + n] = ext[1, first : first + n] * (0.5 / 30.0)
    theta0, weights0 = chebyshev_coefs(DEGREE, FINE_LOW)
    lo, hi = P0 - 4, P0 + 12

    def start_level(level, planes, row, rows, theta, r_in, v_ref, w_ref, make_diagonal, size=2):
        kappa, diagonal, inverse = level
        for first, n in chunks(planes[0], planes[1], size):
            at = (pl.ds(first, n), slice(None), pl.ds(row, rows), slice(None))
            kap = kappa[at]
            if make_diagonal:
                dia = 128.0 * kap + stencil_sum(kappa, first, n, row, rows)
                diagonal[at] = dia
            else:
                dia = diagonal[at]
            inv = jnp.where(kap > 0.0, 1.0 / dia, 0.0)
            inverse[at] = inv
            new = (theta * inv) * r_in(at)
            v_ref[at] = new
            w_ref[at] = kap * new

    level0 = (kap0, dia0, inv0)
    start_level(level0, (lo, hi), 4, 16, theta0, lambda at: ext[(0,) + at], va0, wa0, True)

    def own0(ref):
        return ref[P0 : P0 + 8, 0:2, W0 : W0 + 8, :]

    def put_res0(first, n, r):
        res0[pl.ds(first, n), :, 4:20, :] = r

    xs0[...] = own0(va0)
    here, there = (va0, wa0), (vb0, wb0)

    def smooth0(step, r_in):
        nonlocal here, there
        apply(level0, here, r_in, put_res0, (P0 - 3 + step, P0 + 11 - step), 4, 16, weights0[step], there)
        xs0[...] += own0(there[0])
        here, there = there, here

    smooth0(0, lambda at: ext[(0,) + at])

    k1_arrive()
    for first, n in chunks(0, 12, 2):
        kap1[first : first + n, 0] = kin1[0, first : first + n] * (0.125 / 30.0)
        lane = lanes_of((n, 24, 128))
        halo = jnp.where(lane < 64, kin1[1, first : first + n], kin1[2, first : first + n])
        kap1[first : first + n, 1] = halo * (0.125 / 30.0)
    for first, n in chunks(P1, P1 + 4, 2):
        at = (pl.ds(first, n), slice(None), pl.ds(W1, 8), slice(None))
        value = 128.0 * kap1[at] + stencil_sum(kap1, first, n, W1, 8)
        dia1[first : first + n, :, W1 : W1 + 4, :] = value[:, :, 0:4]
    dia1_arrive = exchange(FLAT, flat1_ends(dia1))
    own_k2 = coarse_of(lambda i, parity, t: kap1[P1 + i, t, pl.ds(W1 + parity, 2, stride=2), :], 2, 2)
    for i, value in enumerate(own_k2):
        kap2[P2 + 2 * mx + i, 0, W2 : W2 + 2, :] = 0.25 * value
    k2_arrive = plane_gather(kap2)

    smooth0(1, lambda at: res0[at])
    smooth0(2, lambda at: res0[at])

    def put_rext(first, n, r):
        rext[pl.ds(first, n), 0:2, W0 : W0 + 8, :] = r[:, 0:2]

    apply(level0, here, lambda at: res0[at], put_rext, (P0, P0 + 8), W0, 8, None)

    own_b1 = coarse_of(lambda i, parity, t: rext[P0 + i, t, pl.ds(W0 + parity, 4, stride=2), :], 4, 4)
    for i, value in enumerate(own_b1):
        bin1[0, P1 + i, W1 : W1 + 4, :] = value
    b1_arrive = exchange(AROUND, level1_ends(bin1))
    pack_edges([lambda i, t: rext[P0 + i, t, W0 : W0 + 8, :]], redge_out)
    redges_arrive = exchange(STACK, edge_ends(redge_out, redge_in))

    def rext_ends(i, j, k):
        (sp, st, sr), (dp, dt, dr) = fine_slices(i, j)
        return rext.at[sp, st, sr, :], rext.at[dp, dt, dr, :]

    rext_arrive = exchange(FLAT, rext_ends)
    dia1_arrive()
    b1_arrive()
    for first, n in chunks(0, 12, 2):
        res1[first : first + n, 0] = bin1[0, first : first + n]
        lane = lanes_of((n, 24, 128))
        res1[first : first + n, 1] = jnp.where(lane < 64, bin1[1, first : first + n], bin1[2, first : first + n])
    level1 = (kap1, dia1, inv1)
    start_level(level1, (0, 12), 4, 16, theta0, lambda at: res1[at], va1, wa1, False)

    def own1(ref):
        return ref[P1 : P1 + 4, :, W1 : W1 + 8, :]

    def put_res1(first, n, r):
        res1[pl.ds(first, n), :, 4:20, :] = r

    xs1[...] = own1(va1)
    here, there = (va1, wa1), (vb1, wb1)
    for step in range(3):
        apply(level1, here, lambda at: res1[at], put_res1, (P1 - 3 + step, P1 + 7 - step), 4, 16, weights0[step], there)
        xs1[...] += own1(there[0])
        here, there = there, here

    def put_rex1(first, n, r):
        rex1[pl.ds(first, n), :, W1 : W1 + 4, :] = r[:, :, 0:4]

    apply(level1, here, lambda at: res1[at], put_rex1, (P1, P1 + 4), W1, 8, None)

    own_b2 = coarse_of(lambda i, parity, t: rex1[P1 + i, t, pl.ds(W1 + parity, 2, stride=2), :], 2, 2)
    for i, value in enumerate(own_b2):
        bin2[P2 + 2 * mx + i, 0, W2 : W2 + 2, :] = value
    b2_arrive = plane_gather(bin2)
    rex1_arrive = exchange(FLAT, flat1_ends(rex1))
    k2_arrive()
    full = 2 * nx
    theta2, weights2 = chebyshev_coefs(COARSE_DEGREE, COARSE_LOW)
    level2 = (kap2, dia2, inv2)
    b2_arrive()
    start_level(level2, (P2, P2 + full), 8, 24, theta2, lambda at: bin2[at], va2, wa2, True)
    window = (slice(P2, P2 + full), slice(None), slice(8, 32), slice(None))
    xs2[window] = va2[window]
    here, there = (va2, wa2), (vb2, wb2)

    def put_res2(first, n, r):
        res2[pl.ds(first, n), :, 8:32, :] = r

    for step in range(COARSE_DEGREE - 1):
        r_in = (lambda at: bin2[at]) if step == 0 else (lambda at: res2[at])
        apply(level2, here, r_in, put_res2, (P2, P2 + full), 8, 24, weights2[step], there)
        xs2[window] += there[0][window]
        here, there = there, here

    half = lanes_of((8, 128)) // 2
    for j in range(6):
        coarse = xs2[P2 + 2 * mx - 2 + j, 0, W2 - 2 : W2 + 6, :]
        for tile in range(2):
            value = pair_gather(coarse, half + 64 * tile)[0:6]
            for e in range(2):
                for parity in range(2):
                    va1[2 * j + e, tile, pl.ds(W1 - 4 + parity, 6, stride=2), :] = value
    for first, n in chunks(0, 12, 2):
        wa1[first : first + n] = kap1[first : first + n] * va1[first : first + n]
    xs1[...] += own1(va1)
    rex1_arrive()
    here, there = (va1, wa1), (vb1, wb1)
    apply(level1, here, lambda at: rex1[at], put_res1, (P1 - 3, P1 + 7), 4, 16, (None, theta0), there)
    xs1[...] += own1(there[0])
    here, there = there, here
    for step in range(3):
        apply(level1, here, lambda at: res1[at], put_res1, (P1 - 2 + step, P1 + 6 - step), 4, 16, weights0[step], there)
        xs1[...] += own1(there[0])
        here, there = there, here
    xex1[P1 : P1 + 4, :, W1 : W1 + 4, :] = xs1[:, :, 0:4, :]
    xex1_arrive = exchange(FLAT, flat1_ends(xex1))

    redges_arrive()

    def put_rext2(p, value):
        rext[p, 2] = value

    unpack_edges(redge_in, 0, put_rext2)
    rext_arrive()
    xex1_arrive()
    lane = lanes_of((8, 128))
    ends = jnp.where(lane < 64, half, half + 64)
    for p in range(1, 11):
        for source_row, keep in ((W1 - 4, 8), (W1 + 4, 4)):
            for tile, source_tile, index in ((0, 0, half), (1, 0, half + 64), (2, 1, ends)):
                value = pair_gather(xex1[p, source_tile, source_row : source_row + 8, :], index)[0:keep]
                for q in (2 * p - 3, 2 * p - 2):
                    if 0 <= q < 18:
                        for parity in range(2):
                            va0[q, tile, pl.ds(2 * (source_row - 4) + parity, keep, stride=2), :] = value
    for first, n in chunks(0, 18, 2):
        wa0[first : first + n] = kap0[first : first + n] * va0[first : first + n]
    xs0[...] += own0(va0)
    here, there = (va0, wa0), (vb0, wb0)
    apply(level0, here, lambda at: rext[at], put_res0, (lo, hi), 4, 16, (None, theta0), there)
    xs0[...] += own0(there[0])
    here, there = there, here
    for step in range(3):
        smooth0(step, lambda at: res0[at])

    def put_out(first, n, r):
        for tile in range(2):
            r_ref[first - P0 : first - P0 + n, :, 128 * tile : 128 * tile + 128] = r[:, tile]

    apply(level0, here, lambda at: res0[at], put_out, (P0, P0 + 8), W0, 8, None)
    for tile in range(2):
        x_ref[:, :, 128 * tile : 128 * tile + 128] = xs0[:, tile]
    for ok, copy in pending:
        pl.when(ok)(copy.wait_send)


def solution(mesh):
    sizes = tuple(mesh.shape[axis] for axis in ("gx", "gy", "gz"))

    def step(conductivity, source):
        def vmem(*shape):
            return pltpu.VMEM(shape, F32)

        level0, level1, level2 = (18, 3, 24, 128), (12, 2, 24, 128), (12, 1, 40, 128)
        sems = 4 * 26 + 3 * 8 + 2 * sizes[0] * SPAN
        shape = jax.ShapeDtypeStruct(conductivity.shape, F32)
        return pl.pallas_call(
            lambda *refs: kernel(sizes, *refs),
            name="cycle",
            out_shape=(shape, shape),
            in_specs=[pl.BlockSpec(memory_space=pltpu.VMEM)] * 2,
            out_specs=(pl.BlockSpec(memory_space=pltpu.VMEM),) * 2,
            scratch_shapes=[
                vmem(2, *level0), vmem(2, 3, 24, 128), vmem(2, 8, 128), vmem(2, 3, 24, 128), vmem(2, 8, 128), vmem(*level0),
                *[vmem(*level0) for _ in range(8)], vmem(8, 2, 8, 128),
                vmem(3, 12, 24, 128), vmem(3, 12, 24, 128), *[vmem(*level1) for _ in range(10)], vmem(4, 2, 8, 128),
                *[vmem(*level2) for _ in range(10)],
                vmem(2, 16, 128), vmem(16, 128),
                pltpu.SemaphoreType.DMA((sems,)), pltpu.SemaphoreType.DMA((sems,)),
            ],
            compiler_params=pltpu.CompilerParams(
                collective_id=0, has_side_effects=True, vmem_limit_bytes=50 * 1024 * 1024
            ),
        )(conductivity, source)

    spec = P("gx", "gy", "gz")
    return jax.shard_map(step, mesh=mesh, in_specs=(spec, spec), out_specs=(spec, spec), check_vma=False)
```

profile of v0, /device:TPU:1, one launch (start us, length us, event | category | flops | bytes accessed | tf_op | source)
XLA Modules:
  0.0 57.1 jit_solution(16932538181810071915)
XLA Ops:
  0.6 0.0 copy-start
  0.6 0.8 %copy-done = f32[8,8,256]{2,1,0:T(8,128)S(1)} copy-done((f32[8,8,256]{2,1,0:T(8,128)S(1)}, f32[8,8,256]{2,1,0:T(8,128)}, u32[]{:S(2)}) %copy-start) | copy-done | bytes 65560
  1.5 0.0 copy-start.1
  1.5 0.8 %copy-done.1 = f32[8,8,256]{2,1,0:T(8,128)S(1)} copy-done((f32[8,8,256]{2,1,0:T(8,128)S(1)}, f32[8,8,256]{2,1,0:T(8,128)}, u32[]{:S(2)}) %copy-start.1) | copy-done | bytes 65560
  2.3 53.5 %cycle.1 = (f32[8,8,256]{2,1,0:T(8,128)S(1)}, f32[8,8,256]{2,1,0:T(8,128)S(1)}) custom-call(f32[8,8,256]{2,1,0:T(8,128)S(1)} %copy-done, f32[8,8,256]{2,1,0:T(8,128)S(1)} %copy-done.1), custom_call_target="tpu_custom_call" | custom-call | tf_op jit(solution)/shard_map/cycle/pallas_call | solution.py:501
  55.9 0.6 %copy.6 = f32[8,8,256]{2,1,0:T(8,128)} copy(f32[8,8,256]{2,1,0:T(8,128)S(1)} %get-tuple-element.4) | data formatting | bytes 131072
  56.5 0.6 %copy.7 = f32[8,8,256]{2,1,0:T(8,128)} copy(f32[8,8,256]{2,1,0:T(8,128)S(1)} %get-tuple-element.5) | data formatting | bytes 131072
Async XLA Ops:
  0.6 0.8 %copy-start = (f32[8,8,256]{2,1,0:T(8,128)S(1)}, f32[8,8,256]{2,1,0:T(8,128)}, u32[]{:S(2)}) copy-start(f32[8,8,256]{2,1,0:T(8,128)} %refs_0_.1) | copy-start | bytes 196612
  1.5 0.8 %copy-start.1 = (f32[8,8,256]{2,1,0:T(8,128)S(1)}, f32[8,8,256]{2,1,0:T(8,128)}, u32[]{:S(2)}) copy-start(f32[8,8,256]{2,1,0:T(8,128)} %refs_1_.1) | copy-start | bytes 196612
where the time goes:
time: 57.9 us; the launch traced here: 57.1 us
  Pallas kernels  53.5 us (92%)
  local copies, waits for them, and re-layouts  2.93 us (5%)
  between operations  0.65 us (1%)
    pallas_call x1, Pallas kernels, step(): pl.pallas_call(lambda *refs: kernel(sizes, *refs), name='cycle', out_shap...  53.5 us
    unnamed x6, local copies, waits for them, and re-layouts  2.93 us

commit v1 on v0

v1 whole, which is shorter than its diff:
```python
import jax
import jax.numpy as jnp
from jax import lax
from jax.experimental import pallas as pl
from jax.experimental.pallas import tpu as pltpu
from jax.sharding import PartitionSpec as P

MESH = pl.DeviceIdType.MESH
F32 = jnp.float32
DEGREE = 4
COARSE_DEGREE = 8
UPPER = 2.0
FINE_LOW = 0.5
COARSE_LOW = 0.03
REACH = 5

P0, W0 = 5, 8
P1, W1 = 4, 8
P2, W2 = 2, 18
SIDES = (-1, 0, 1)
FLAT = [(i, j, 0) for i in SIDES for j in SIDES if (i, j) != (0, 0)]
STACK = [(i, j, k) for k in (-1, 1) for i in SIDES for j in SIDES]
DIAGONAL_FIRST = sorted(FLAT, key=lambda o: -abs(o[0]) - abs(o[1]))


def chebyshev_coefs(degree, lower):
    centre = (UPPER + lower) / 2.0
    half_width = (UPPER - lower) / 2.0
    ratio_term = centre / half_width
    rho_prev = 1.0 / ratio_term
    weights = []
    for _ in range(1, degree):
        rho_next = 1.0 / (2.0 * ratio_term - rho_prev)
        weights.append((rho_next * rho_prev, 2.0 * rho_next / half_width))
        rho_prev = rho_next
    return 1.0 / centre, weights


def rolled(values, shift):
    flat = values.reshape(-1, 128)
    return pltpu.roll(flat, shift % 128, 1).reshape(values.shape)


def lanes_of(shape):
    return lax.broadcasted_iota(jnp.int32, shape, len(shape) - 1)


def beside(values):
    up, down = rolled(values, 1), rolled(values, -1)
    tiles = values.shape[1]
    if tiles > 1:
        lane = lanes_of(values.shape)
        before = jnp.concatenate([up[:, tiles - 1 :], up[:, : tiles - 1]], axis=1)
        after = jnp.concatenate([down[:, 1:], down[:, :1]], axis=1)
        up = jnp.where(lane == 0, before, up)
        down = jnp.where(lane == 127, after, down)
    return up + down


def stencil_sum(ref, first, count, row, rows):
    planes = pl.ds(first - 1, count + 2)
    centre = ref[planes, :, pl.ds(row, rows), :]
    side = ref[planes, :, pl.ds(row - 1, rows), :] + ref[planes, :, pl.ds(row + 1, rows), :]
    corner = 3.0 * centre + side
    face = 14.0 * centre + 3.0 * side
    outer = face[1:-1] + corner[:-2] + corner[2:]
    middle = 14.0 * side[1:-1] + face[:-2] + face[2:]
    return middle + beside(outer)


def chunks(first, last, size):
    return [(at, min(size, last - at)) for at in range(first, last, size)]


def apply(level, source, r_in, r_out, planes, row, rows, coefs, target=None, size=2):
    kappa, diagonal, inverse = level
    v_ref, w_ref = source
    for first, count in chunks(planes[0], planes[1], size):
        at = (pl.ds(first, count), slice(None), pl.ds(row, rows), slice(None))
        v = v_ref[at]
        r = r_in(at) - diagonal[at] * v
        r = r + kappa[at] * stencil_sum(v_ref, first, count, row, rows)
        r = r + stencil_sum(w_ref, first, count, row, rows)
        if r_out is not None:
            r_out(first, count, r)
        if coefs is not None:
            new = (coefs[1] * inverse[at]) * r
            if coefs[0] is not None:
                new = new + coefs[0] * v
            target[0][at] = new
            target[1][at] = kappa[at] * new


def pair_gather(values, index):
    return jnp.take_along_axis(values, index, axis=1)


def kernel(sizes, k_ref, b_ref, x_ref, r_ref, ext, edge_in, edge_out, redge_in, redge_out, rext,
           kap0, dia0, inv0, res0, va0, wa0, vb0, wb0, xs0,
           kin1, bin1, kedge_in, kedge_out, bedge_in, bedge_out, kap1, dia1, inv1, res1, va1, wa1, vb1, wb1, rex1, xex1, xs1,
           kin2, kap2, dia2, inv2, bin2, res2, va2, wa2, vb2, wb2, xs2, tmp, tmp2, spare, send, recv, load):
    nx, ny, nz = sizes
    mx, my, mz = lax.axis_index("gx"), lax.axis_index("gy"), lax.axis_index("gz")
    used = [0]

    def inside(i, j, k):
        tests = []
        if i < 0:
            tests.append(mx + i >= 0)
        if i > 0:
            tests.append(mx + i < nx)
        if j < 0:
            tests.append(my + j >= 0)
        if j > 0:
            tests.append(my + j < ny)
        if k < 0:
            tests.append(mz + k >= 0)
        if k > 0:
            tests.append(mz + k < nz)
        ok = tests[0]
        for test in tests[1:]:
            ok = ok & test
        return ok

    def amount(where, rows, number, sent):
        whole = spare.at[pl.ds(0, rows)]

        @pl.when(where)
        def _():
            copy = pltpu.make_async_remote_copy(
                src_ref=whole, dst_ref=whole, send_sem=send.at[number], recv_sem=recv.at[number],
                device_id=(mx, my, mz), device_id_type=MESH,
            )
            if sent:
                copy.wait_send()
            else:
                copy.wait_recv()

    def waits(number, cases):
        def wait(sent):
            with jax.named_scope(f"{'sent' if sent else 'wait'}{number}"):
                for where, rows in cases:
                    amount(where, rows, number, sent)

        return (lambda: wait(False)), (lambda: wait(True))

    def some(n):
        return (1, 2) if n > 2 else (1,)

    near_x = jnp.where(mx > 0, 1, 0) + jnp.where(mx < nx - 1, 1, 0)
    near_y = jnp.where(my > 0, 1, 0) + jnp.where(my < ny - 1, 1, 0)
    near_z = jnp.where(mz > 0, 1, 0) + jnp.where(mz < nz - 1, 1, 0)
    low_y, high_y = jnp.minimum(my, REACH), jnp.minimum(ny - 1 - my, REACH)
    far_counts = sorted({min(y, REACH) + min(ny - 1 - y, REACH) for y in range(ny)})

    def exchange(moves, face, corner, stack):
        number = used[0]
        used[0] += 1
        for (i, j, k), src, dst in moves:
            copy = pltpu.make_async_remote_copy(
                src_ref=src, dst_ref=dst, send_sem=send.at[number], recv_sem=recv.at[number],
                device_id=(mx + i, my + j, mz + k), device_id_type=MESH,
            )
            pl.when(inside(i, j, k))(copy.start)
        cases = []
        for x in some(nx):
            for y in some(ny):
                for z in some(nz) if stack else (0,):
                    where = (near_x == x) & (near_y == y)
                    if stack:
                        where = where & (near_z == z)
                    cases.append((where, (x + y) * face + x * y * corner + z * (1 + x) * (1 + y) * stack))
        return waits(number, cases)

    def mine(ref):
        return ref.at[pl.ds(P2 + 2 * mx, 2), :, pl.ds(W2, 2), :]

    def far_start(ref, number, shift, j):
        copy = pltpu.make_async_remote_copy(
            src_ref=mine(ref), dst_ref=ref.at[pl.ds(P2 + 2 * mx, 2), :, pl.ds(W2 - 2 * j, 2), :],
            send_sem=send.at[number], recv_sem=recv.at[number],
            device_id=(lax.rem(mx + shift, nx), my + j, mz), device_id_type=MESH,
        )
        if j == 0:
            copy.start()
        else:
            pl.when(inside(0, j, 0))(copy.start)

    distances = [j for j in sorted(range(-REACH, REACH + 1), key=lambda o: -abs(o)) if abs(j) < ny]

    def column_gather(ref):
        number = used[0]
        used[0] += 1
        for j in distances:
            if j != 0:
                far_start(ref, number, 0, j)
        return waits(number, [(low_y + high_y == c, 4 * c) for c in far_counts])

    def plane_gather(ref):
        number = used[0]
        used[0] += 1
        for j in distances:
            for shift in range(nx):
                if (shift, j) != (0, 0):
                    far_start(ref, number, shift, j)
        return waits(number, [(low_y + high_y == c, 4 * ((1 + c) * nx - 1)) for c in far_counts])

    def row_gather(ref):
        number = used[0]
        used[0] += 1
        part = ref.at[pl.ds(P2 + 2 * mx, 2), :, pl.ds(W2 - 2 * REACH, 4 * REACH + 2), :]
        for shift in range(1, nx):
            pltpu.make_async_remote_copy(
                src_ref=part, dst_ref=part, send_sem=send.at[number], recv_sem=recv.at[number],
                device_id=(lax.rem(mx + shift, nx), my, mz), device_id_type=MESH,
            ).start()
        return waits(number, [(mx >= 0, (nx - 1) * 2 * (4 * REACH + 2))])

    def zero(ref):
        ref[...] = jnp.zeros(ref.shape, F32)

    def coarse_of(read, count, rows):
        for tile in range(2):
            for i in range(count):
                total = read(2 * i, 0, tile) + read(2 * i, 1, tile) + read(2 * i + 1, 0, tile) + read(2 * i + 1, 1, tile)
                tmp[tile, rows * i : rows * (i + 1), :] = 0.125 * total
        size = max(8, count * rows)
        lane = lanes_of((size, 128))
        pairs = [tmp[tile, 0:size, :] for tile in range(2)]
        pairs = [p + pltpu.roll(p, 127, 1) for p in pairs]
        index = (2 * lane) % 128
        out = jnp.where(lane < 64, pair_gather(pairs[0], index), pair_gather(pairs[1], index))
        tmp2[0:size, :] = out
        return [tmp2[rows * i : rows * (i + 1), :] for i in range(count)]

    def pack_edges(reads, out):
        for way, (tile, start) in enumerate(((1, 120), (0, 0))):
            packed = jnp.zeros((8, 128), F32)
            lane = lanes_of((8, 128))
            for a, read in enumerate(reads):
                for i in range(8):
                    at = 8 * i + 64 * a
                    part = pltpu.roll(read(i, tile), (at - start) % 128, 1)
                    packed = jnp.where((lane >= at) & (lane < at + 8), part, packed)
            out[way] = packed

    def edge_moves(src, dst, width):
        moves = []
        for i, j, k in STACK:
            way, side = (0, 0) if k > 0 else (1, 1)
            own = W0 if width == 8 else W1
            to = dst.at[side, 1 - i, pl.ds(own - width * j, width), :]
            moves.append(((i, j, k), src.at[way, pl.ds(0, width), :], to))
        return moves

    def pack_coarse(out):
        lane = lanes_of((4, 128))
        for way, start in enumerate((96, 0)):
            packed = jnp.zeros((4, 128), F32)
            for i in range(4):
                part = pltpu.roll(tmp2[4 * i : 4 * i + 8, :], (32 * i - start) % 128, 1)[0:4]
                packed = jnp.where((lane >= 32 * i) & (lane < 32 * i + 32), part, packed)
            out[way, 0:4] = packed

    def unpack_coarse(src, p):
        lane = lanes_of((24, 128))
        high_end, low_start = jnp.where(mz < nz - 1, 32, 0), jnp.where(mz > 0, 96, 128)
        low = pltpu.roll(src[0, p // 4], (96 - 32 * (p % 4)) % 128, 1)
        high = pltpu.roll(src[1, p // 4], (-32 * (p % 4)) % 128, 1)
        return jnp.where(lane < high_end, high, jnp.where(lane >= low_start, low, 0.0))

    def unpack_edges(src, a, write):
        lane = lanes_of((24, 128))
        high_end, low_start = jnp.where(mz < nz - 1, 8, 0), jnp.where(mz > 0, 120, 128)
        for p in range(2 * P0 + 8):
            group, i = (0, 3 + p) if p < P0 else ((1, p - P0) if p < P0 + 8 else (2, p - P0 - 8))
            at = 8 * i + 64 * a
            low = pltpu.roll(src[0, group], (120 - at) % 128, 1)
            high = pltpu.roll(src[1, group], -at % 128, 1)
            write(p, jnp.where(lane < high_end, high, jnp.where(lane >= low_start, low, 0.0)))

    def halo(step, own, width, depth):
        if step == 0:
            return pl.ds(own, width), pl.ds(own, width)
        if step > 0:
            return pl.ds(own + width - depth, depth), pl.ds(own - depth, depth)
        return pl.ds(own, depth), pl.ds(own + width, depth)

    def fine_moves(ref, depth):
        moves = []
        for i, j, k in DIAGONAL_FIRST:
            (sp, dp), (sr, dr) = halo(i, P0, 8, depth), halo(j, W0, 8, depth)
            moves.append(((i, j, k), ref.at[sp, pl.ds(0, 2), sr, :], ref.at[dp, pl.ds(0, 2), dr, :]))
        return moves

    def coarse_moves(ref, depth, tiles):
        moves = []
        for i, j, k in DIAGONAL_FIRST:
            (sp, dp), (sr, dr) = halo(i, P1, 4, depth), halo(j, W1, 4, depth)
            if tiles:
                moves.append(((i, j, k), ref.at[sp, :, sr, :], ref.at[dp, :, dr, :]))
            else:
                moves.append(((i, j, k), ref.at[sp, sr, :], ref.at[dp, dr, :]))
        return moves

    loads = []
    for a, source in enumerate((b_ref, k_ref)):
        for tile in range(2):
            loads.append(
                pltpu.make_async_copy(
                    source.at[:, :, pl.ds(128 * tile, 128)],
                    ext.at[a, pl.ds(P0, 8), tile, pl.ds(W0, 8), :],
                    load.at[2 * a + tile],
                )
            )
            loads[-1].start()
    barrier = pltpu.get_barrier_semaphore()

    def greet(ok, i, j, k):
        @pl.when(ok)
        def _():
            pl.semaphore_signal(barrier, inc=1, device_id=(i, j, k), device_id_type=MESH)

        return jnp.where(ok, 1, 0)

    count = 0
    for j in range(-REACH, REACH + 1):
        if abs(j) < ny:
            for gx in range(nx):
                count = count + greet(gx != mx if j == 0 else inside(0, j, 0), gx, my + j, mz)
    for i, j, k in STACK:
        count = count + greet(inside(i, j, k), mx + i, my + j, mz + k)
    for copy in loads:
        copy.wait()
    zero(tmp)
    zero(tmp2)
    pack_edges([lambda i, t: ext[0, P0 + i, t, W0 : W0 + 8, :], lambda i, t: ext[1, P0 + i, t, W0 : W0 + 8, :]], edge_out)
    with jax.named_scope("barrier"):
        pl.semaphore_wait(barrier, count)
    moves = edge_moves(edge_out, edge_in, 8)
    for (offset, src_b, dst_b), (_, src_k, dst_k) in zip(fine_moves(ext.at[0], 4), fine_moves(ext.at[1], 5)):
        moves += [(offset, src_b, dst_b), (offset, src_k, dst_k)]
    x0_arrive, x0_left = exchange(moves, 144, 82, 8)

    for ref in (redge_in, rext, bin1, bedge_in, dia1, rex1, xex1):
        zero(ref)
    own_k1 = coarse_of(lambda i, parity, t: ext[1, P0 + i, t, pl.ds(W0 + parity, 4, stride=2), :], 4, 4)
    for i, value in enumerate(own_k1):
        kin1[P1 + i, W1 : W1 + 4, :] = value
    pack_coarse(kedge_out)
    k1_arrive, k1_left = exchange(edge_moves(kedge_out, kedge_in, 4) + coarse_moves(kin1, 4, False), 16, 16, 4)
    for ref in (va0, wa0, vb0, wb0, va1, wa1, vb1, wb1, kap2, va2, wa2, vb2, wb2, xs2):
        zero(ref)
    x0_arrive()

    def put(a):
        def write(p, value):
            ext[a, p, 2] = value

        return write

    unpack_edges(edge_in, 0, put(0))
    unpack_edges(edge_in, 1, put(1))
    row = lax.broadcasted_iota(jnp.int32, (24, 128), 0)

    def planes_in(p, own, width):
        return (mx > 0) if p < own else ((mx < nx - 1) if p >= own + width else None)

    def inside_rows(p, own, width, own_row, width_row, depth):
        start = jnp.where(my > 0, own_row - depth, own_row)
        stop = jnp.where(my < ny - 1, own_row + width_row + depth, own_row + width_row)
        ok = planes_in(p, own, width)
        if ok is not None:
            stop = jnp.where(ok, stop, 0)
        return (row >= start) & (row < stop)

    for p in range(18):
        mask = inside_rows(p, P0, 8, W0, 8, 5)
        for tile in range(3):
            kap0[p, tile] = jnp.where(mask, ext[1, p, tile] * (0.5 / 30.0), 0.0)
    theta0, weights0 = chebyshev_coefs(DEGREE, FINE_LOW)
    lo, hi = P0 - 4, P0 + 12

    def start_level(level, planes, row, rows, theta, r_in, r_out, v_ref, w_ref, make_diagonal, size=2):
        kappa, diagonal, inverse = level
        for first, n in chunks(planes[0], planes[1], size):
            at = (pl.ds(first, n), slice(None), pl.ds(row, rows), slice(None))
            kap = kappa[at]
            if make_diagonal:
                dia = 128.0 * kap + stencil_sum(kappa, first, n, row, rows)
                diagonal[at] = dia
            else:
                dia = diagonal[at]
            inv = jnp.where(kap > 0.0, 1.0 / dia, 0.0)
            inverse[at] = inv
            r = jnp.where(kap > 0.0, r_in(at), 0.0)
            r_out[at] = r
            new = (theta * inv) * r
            v_ref[at] = new
            w_ref[at] = kap * new

    level0 = (kap0, dia0, inv0)
    start_level(level0, (lo, hi), 4, 16, theta0, lambda at: ext[(0,) + at], res0, va0, wa0, True)

    def own0(ref):
        return ref[P0 : P0 + 8, 0:2, W0 : W0 + 8, :]

    def put_res0(first, n, r):
        res0[pl.ds(first, n), :, 4:20, :] = r

    xs0[...] = own0(va0)
    here, there = (va0, wa0), (vb0, wb0)

    def smooth0(step, r_in):
        nonlocal here, there
        apply(level0, here, r_in, put_res0, (P0 - 3 + step, P0 + 11 - step), 4, 16, weights0[step], there)
        xs0[...] += own0(there[0])
        here, there = there, here

    smooth0(0, lambda at: res0[at])
    smooth0(1, lambda at: res0[at])

    k1_arrive()
    for p in range(12):
        mask = inside_rows(p, P1, 4, W1, 4, 4)
        kap1[p, 0] = jnp.where(mask, kin1[p] * (0.125 / 30.0), 0.0)
        kap1[p, 1] = jnp.where(mask, unpack_coarse(kedge_in, p) * (0.125 / 30.0), 0.0)
    for first, n in chunks(P1, P1 + 4, 2):
        at = (pl.ds(first, n), slice(None), pl.ds(W1, 8), slice(None))
        value = 128.0 * kap1[at] + stencil_sum(kap1, first, n, W1, 8)
        dia1[first : first + n, :, W1 : W1 + 4, :] = value[:, :, 0:4]
    d1_arrive, d1_left = exchange(coarse_moves(dia1, 4, True), 32, 32, 0)
    own_k2 = coarse_of(lambda i, parity, t: kap1[P1 + i, t, pl.ds(W1 + parity, 2, stride=2), :], 2, 2)
    for i, value in enumerate(own_k2):
        kin2[P2 + 2 * mx + i, 0, W2 : W2 + 2, :] = 0.25 * value
    k2_arrive, k2_left = column_gather(kin2)
    smooth0(2, lambda at: res0[at])

    def put_rext(first, n, r):
        rext[0, pl.ds(first, n), 0:2, W0 : W0 + 8, :] = r[:, 0:2]

    apply(level0, here, lambda at: res0[at], put_rext, (P0, P0 + 8), W0, 8, None)

    own_b1 = coarse_of(lambda i, parity, t: rext[0, P0 + i, t, pl.ds(W0 + parity, 4, stride=2), :], 4, 4)
    for i, value in enumerate(own_b1):
        bin1[P1 + i, W1 : W1 + 4, :] = value
    pack_coarse(bedge_out)
    b1_arrive, b1_left = exchange(edge_moves(bedge_out, bedge_in, 4) + coarse_moves(bin1, 4, False), 16, 16, 4)
    pack_edges([lambda i, t: rext[0, P0 + i, t, W0 : W0 + 8, :]], redge_out)
    x0_left()
    k1_left()
    d1_arrive()
    d1_left()
    b1_arrive()
    for p in range(12):
        res1[p, 0] = bin1[p]
        res1[p, 1] = unpack_coarse(bedge_in, p)
    level1 = (kap1, dia1, inv1)
    start_level(level1, (0, 12), 4, 16, theta0, lambda at: res1[at], res1, va1, wa1, False)

    def own1(ref):
        return ref[P1 : P1 + 4, :, W1 : W1 + 8, :]

    def put_res1(first, n, r):
        res1[pl.ds(first, n), :, 4:20, :] = r

    xs1[...] = own1(va1)
    here, there = (va1, wa1), (vb1, wb1)
    for step in range(3):
        apply(level1, here, lambda at: res1[at], put_res1, (P1 - 3 + step, P1 + 7 - step), 4, 16, weights0[step], there)
        xs1[...] += own1(there[0])
        here, there = there, here

    def put_rex1(first, n, r):
        rex1[pl.ds(first, n), :, W1 : W1 + 4, :] = r[:, :, 0:4]

    apply(level1, here, lambda at: res1[at], put_rex1, (P1, P1 + 4), W1, 8, None)

    own_b2 = coarse_of(lambda i, parity, t: rex1[P1 + i, t, pl.ds(W1 + parity, 2, stride=2), :], 2, 2)
    for i, value in enumerate(own_b2):
        bin2[P2 + 2 * mx + i, 0, W2 : W2 + 2, :] = value
    b2_arrive, b2_left = plane_gather(bin2)
    r1_arrive, r1_left = exchange(coarse_moves(rex1, 3, True), 24, 18, 0)
    k2_arrive()
    m2_arrive, m2_left = row_gather(kin2)
    k2_left()
    b1_left()
    m2_arrive()
    m2_left()
    full = 2 * nx
    at_row = lax.broadcasted_iota(jnp.int32, (full, 1, 24, 128), 2) + (8 - W2)
    start, stop = jnp.maximum(-2 * REACH, -2 * my), jnp.minimum(2 * REACH + 2, 2 * (ny - my))
    window = (slice(P2, P2 + full), slice(None), slice(8, 32), slice(None))
    kap2[window] = jnp.where((at_row >= start) & (at_row < stop), kin2[window], 0.0)
    theta2, weights2 = chebyshev_coefs(COARSE_DEGREE, COARSE_LOW)
    level2 = (kap2, dia2, inv2)
    b2_arrive()
    r0_arrive, r0_left = exchange(edge_moves(redge_out, redge_in, 8) + fine_moves(rext.at[0], 4), 64, 32, 8)
    start_level(level2, (P2, P2 + full), 8, 24, theta2, lambda at: bin2[at], res2, va2, wa2, True)
    xs2[window] = va2[window]
    here, there = (va2, wa2), (vb2, wb2)

    def put_res2(first, n, r):
        res2[pl.ds(first, n), :, 8:32, :] = r

    for step in range(COARSE_DEGREE - 1):
        apply(level2, here, lambda at: res2[at], put_res2, (P2, P2 + full), 8, 24, weights2[step], there)
        xs2[window] += there[0][window]
        here, there = there, here

    half = lanes_of((8, 128)) // 2
    for j in range(6):
        coarse = xs2[P2 + 2 * mx - 2 + j, 0, W2 - 2 : W2 + 6, :]
        for tile in range(2):
            value = pair_gather(coarse, half + 64 * tile)[0:6]
            for e in range(2):
                for parity in range(2):
                    va1[2 * j + e, tile, pl.ds(W1 - 4 + parity, 6, stride=2), :] = value
    for first, n in chunks(0, 12, 2):
        wa1[first : first + n] = kap1[first : first + n] * va1[first : first + n]
    xs1[...] += own1(va1)
    r1_arrive()
    here, there = (va1, wa1), (vb1, wb1)
    apply(level1, here, lambda at: rex1[at], put_res1, (P1 - 3, P1 + 7), 4, 16, (None, theta0), there)
    xs1[...] += own1(there[0])
    here, there = there, here
    for step in range(3):
        apply(level1, here, lambda at: res1[at], put_res1, (P1 - 2 + step, P1 + 6 - step), 4, 16, weights0[step], there)
        xs1[...] += own1(there[0])
        here, there = there, here
    xex1[P1 : P1 + 4, :, W1 : W1 + 4, :] = xs1[:, :, 0:4, :]
    x1_arrive, x1_left = exchange(coarse_moves(xex1, 3, True), 24, 18, 0)
    b2_left()
    r1_left()
    r0_left()
    r0_arrive()

    def put_rext2(p, value):
        rext[0, p, 2] = value

    unpack_edges(redge_in, 0, put_rext2)
    x1_arrive()
    lane = lanes_of((8, 128))
    ends = jnp.where(lane < 64, half, half + 64)
    for p in range(1, 11):
        for source_row, keep in ((W1 - 4, 8), (W1 + 4, 4)):
            for tile, source_tile, index in ((0, 0, half), (1, 0, half + 64), (2, 1, ends)):
                value = pair_gather(xex1[p, source_tile, source_row : source_row + 8, :], index)[0:keep]
                for q in (2 * p - 3, 2 * p - 2):
                    if 0 <= q < 18:
                        for parity in range(2):
                            va0[q, tile, pl.ds(2 * (source_row - 4) + parity, keep, stride=2), :] = value
    for first, n in chunks(0, 18, 2):
        wa0[first : first + n] = kap0[first : first + n] * va0[first : first + n]
    xs0[...] += own0(va0)
    here, there = (va0, wa0), (vb0, wb0)
    apply(level0, here, lambda at: rext[(0,) + at], put_res0, (lo, hi), 4, 16, (None, theta0), there)
    xs0[...] += own0(there[0])
    here, there = there, here
    for step in range(3):
        smooth0(step, lambda at: res0[at])

    def put_out(first, n, r):
        for tile in range(2):
            r_ref[first - P0 : first - P0 + n, :, 128 * tile : 128 * tile + 128] = r[:, tile]

    apply(level0, here, lambda at: res0[at], put_out, (P0, P0 + 8), W0, 8, None)
    for tile in range(2):
        x_ref[:, :, 128 * tile : 128 * tile + 128] = xs0[:, tile]
    x1_left()


def solution(mesh):
    sizes = tuple(mesh.shape[axis] for axis in ("gx", "gy", "gz"))

    def step(conductivity, source):
        def vmem(*shape):
            return pltpu.VMEM(shape, F32)

        level0, level1, level2 = (18, 3, 24, 128), (12, 2, 24, 128), (12, 1, 40, 128)
        sems = 10
        shape = jax.ShapeDtypeStruct(conductivity.shape, F32)
        return pl.pallas_call(
            lambda *refs: kernel(sizes, *refs),
            name="cycle",
            out_shape=(shape, shape),
            in_specs=[pl.BlockSpec(memory_space=pltpu.HBM)] * 2,
            out_specs=(pl.BlockSpec(memory_space=pltpu.VMEM),) * 2,
            scratch_shapes=[
                vmem(2, *level0), vmem(2, 3, 24, 128), vmem(2, 8, 128), vmem(2, 3, 24, 128), vmem(2, 8, 128), vmem(1, *level0),
                *[vmem(*level0) for _ in range(8)], vmem(8, 2, 8, 128),
                vmem(12, 24, 128), vmem(12, 24, 128), *[vmem(*s) for s in 2 * ((2, 3, 24, 128), (2, 8, 128))], *[vmem(*level1) for _ in range(10)], vmem(4, 2, 8, 128),
                *[vmem(*level2) for _ in range(11)],
                vmem(2, 16, 128), vmem(24, 128), vmem(1152, 128),
                pltpu.SemaphoreType.DMA((sems,)), pltpu.SemaphoreType.DMA((sems,)), pltpu.SemaphoreType.DMA((4,)),
            ],
            compiler_params=pltpu.CompilerParams(
                collective_id=0, has_side_effects=True, vmem_limit_bytes=50 * 1024 * 1024
            ),
        )(*(pltpu.with_memory_space_constraint(v, pltpu.HBM) for v in (conductivity, source)))

    spec = P("gx", "gy", "gz")
    return jax.shard_map(step, mesh=mesh, in_specs=(spec, spec), out_specs=(spec, spec), check_vma=False)
```

time: 57.9 us -> 48.3 us (0.83); the launches traced: 57.1 us -> 48.1 us
  Pallas kernels: 53.5 us -> 46.2 us
  local copies, waits for them, and re-layouts: 2.93 us -> 1.26 us
    pallas_call x1, Pallas kernels: 53.5 us -> 46.2 us  [step(): pl.pallas_call(lambda *refs: kernel(sizes, *refs), name='cycle', out_shap...]
    unnamed x6 -> x2, local copies, waits for them, and re-layouts: 2.93 us -> 1.26 us
where the time goes in v1:
time: 48.3 us; the launch traced here: 48.1 us
  Pallas kernels  46.2 us (96%)
  local copies, waits for them, and re-layouts  1.26 us (3%)
  between operations  0.64 us (1%)
    pallas_call x1, Pallas kernels, step(): pl.pallas_call(lambda *refs: kernel(sizes, *refs), name='cycle', out_shap...  46.2 us
    unnamed x2, local copies, waits for them, and re-layouts  1.26 us

profile of v1, /device:TPU:1, one launch (start us, length us, event | category | flops | bytes accessed | tf_op | source)
XLA Modules:
  0.0 48.1 jit_solution(305468623111643106)
XLA Ops:
  0.6 46.2 %cycle.1 = (f32[8,8,256]{2,1,0:T(8,128)S(1)}, f32[8,8,256]{2,1,0:T(8,128)S(1)}) custom-call(f32[8,8,256]{2,1,0:T(8,128)} %refs_0_.1, f32[8,8,256]{2,1,0:T(8,128)} %refs_1_.1), custom_call_target="tpu_custom_call" | custom-call | tf_op jit(solution)/shard_map/cycle/pallas_call | solution.py:583
  46.9 0.6 %copy.6 = f32[8,8,256]{2,1,0:T(8,128)} copy(f32[8,8,256]{2,1,0:T(8,128)S(1)} %get-tuple-element.4) | data formatting | bytes 131072
  47.5 0.6 %copy.7 = f32[8,8,256]{2,1,0:T(8,128)} copy(f32[8,8,256]{2,1,0:T(8,128)S(1)} %get-tuple-element.5) | data formatting | bytes 131072

commit v2 on v1

--- a/solution.py
+++ b/solution.py
@@ -18,8 +18,10 @@
 P1, W1 = 4, 8
 P2, W2 = 2, 18
 SIDES = (-1, 0, 1)
+FINE = 7
 FLAT = [(i, j, 0) for i in SIDES for j in SIDES if (i, j) != (0, 0)]
 STACK = [(i, j, k) for k in (-1, 1) for i in SIDES for j in SIDES]
+NEXT, OVER = [(0, -1, 0), (0, 1, 0)], [(0, -2, 0), (0, 2, 0)]
 DIAGONAL_FIRST = sorted(FLAT, key=lambda o: -abs(o[0]) - abs(o[1]))
 
 
@@ -81,8 +83,10 @@
         r = r_in(at) - diagonal[at] * v
         r = r + kappa[at] * stencil_sum(v_ref, first, count, row, rows)
         r = r + stencil_sum(w_ref, first, count, row, rows)
-        if r_out is not None:
+        if callable(r_out):
             r_out(first, count, r)
+        else:
+            r_out[at] = r
         if coefs is not None:
             new = (coefs[1] * inverse[at]) * r
             if coefs[0] is not None:
@@ -98,7 +102,7 @@
 def kernel(sizes, k_ref, b_ref, x_ref, r_ref, ext, edge_in, edge_out, redge_in, redge_out, rext,
            kap0, dia0, inv0, res0, va0, wa0, vb0, wb0, xs0,
            kin1, bin1, kedge_in, kedge_out, bedge_in, bedge_out, kap1, dia1, inv1, res1, va1, wa1, vb1, wb1, rex1, xex1, xs1,
-           kin2, kap2, dia2, inv2, bin2, res2, va2, wa2, vb2, wb2, xs2, tmp, tmp2, spare, send, recv, load):
+           kin2, kap2, dia2, inv2, bin2, res2, va2, wa2, vb2, wb2, xs2, tmp, tmp2, spare, send, recv, load, news):
     nx, ny, nz = sizes
     mx, my, mz = lax.axis_index("gx"), lax.axis_index("gy"), lax.axis_index("gz")
     used = [0]
@@ -169,7 +173,7 @@
                     where = (near_x == x) & (near_y == y)
                     if stack:
                         where = where & (near_z == z)
-                    cases.append((where, (x + y) * face + x * y * corner + z * (1 + x) * (1 + y) * stack))
+                    cases.append((where, (x + y) * face + x * y * corner + (z * (1 + x) * (stack[0] + y * stack[1]) if stack else 0)))
         return waits(number, cases)
 
     def mine(ref):
@@ -244,13 +248,13 @@
                     packed = jnp.where((lane >= at) & (lane < at + 8), part, packed)
             out[way] = packed
 
-    def edge_moves(src, dst, width):
+    def edge_moves(src, dst, own, width, depth):
         moves = []
         for i, j, k in STACK:
             way, side = (0, 0) if k > 0 else (1, 1)
-            own = W0 if width == 8 else W1
-            to = dst.at[side, 1 - i, pl.ds(own - width * j, width), :]
-            moves.append(((i, j, k), src.at[way, pl.ds(0, width), :], to))
+            rows, there = halo(j, own, width, depth)
+            mine_rows = pl.ds(rows.start - own, rows.size)
+            moves.append(((i, j, k), src.at[way, mine_rows, :], dst.at[side, 1 - i, there, :]))
         return moves
 
     def pack_coarse(out):
@@ -316,31 +320,30 @@
             loads[-1].start()
     barrier = pltpu.get_barrier_semaphore()
 
-    def greet(ok, i, j, k):
-        @pl.when(ok)
-        def _():
-            pl.semaphore_signal(barrier, inc=1, device_id=(i, j, k), device_id_type=MESH)
-
-        return jnp.where(ok, 1, 0)
-
-    count = 0
-    for j in range(-REACH, REACH + 1):
-        if abs(j) < ny:
-            for gx in range(nx):
-                count = count + greet(gx != mx if j == 0 else inside(0, j, 0), gx, my + j, mz)
-    for i, j, k in STACK:
-        count = count + greet(inside(i, j, k), mx + i, my + j, mz + k)
+    def tell(offsets, semaphore):
+        for i, j, k in offsets:
+
+            @pl.when(inside(i, j, k))
+            def _():
+                pl.semaphore_signal(semaphore, inc=1, device_id=(mx + i, my + j, mz + k), device_id_type=MESH)
+
+    def hear(offsets, semaphore):
+        with jax.named_scope("hear"):
+            pl.semaphore_wait(semaphore, sum(jnp.where(inside(i, j, k), 1, 0) for i, j, k in offsets))
+
+    tell(STACK + FLAT, barrier)
+    zero(tmp)
+    zero(tmp2)
     for copy in loads:
         copy.wait()
-    zero(tmp)
-    zero(tmp2)
     pack_edges([lambda i, t: ext[0, P0 + i, t, W0 : W0 + 8, :], lambda i, t: ext[1, P0 + i, t, W0 : W0 + 8, :]], edge_out)
-    with jax.named_scope("barrier"):
-        pl.semaphore_wait(barrier, count)
-    moves = edge_moves(edge_out, edge_in, 8)
+    hear(STACK + FLAT, barrier)
+    moves = edge_moves(edge_out, edge_in, W0, 8, 5)
     for (offset, src_b, dst_b), (_, src_k, dst_k) in zip(fine_moves(ext.at[0], 4), fine_moves(ext.at[1], 5)):
         moves += [(offset, src_b, dst_b), (offset, src_k, dst_k)]
-    x0_arrive, x0_left = exchange(moves, 144, 82, 8)
+    x0_arrive, x0_left = exchange(moves, 144, 82, (8, 5))
+
+    tell(NEXT, news.at[0])
 
     for ref in (redge_in, rext, bin1, bedge_in, dia1, rex1, xex1):
         zero(ref)
@@ -348,11 +351,14 @@
     for i, value in enumerate(own_k1):
         kin1[P1 + i, W1 : W1 + 4, :] = value
     pack_coarse(kedge_out)
-    k1_arrive, k1_left = exchange(edge_moves(kedge_out, kedge_in, 4) + coarse_moves(kin1, 4, False), 16, 16, 4)
+    k1_arrive, k1_left = exchange(edge_moves(kedge_out, kedge_in, W1, 4, 4) + coarse_moves(kin1, 4, False), 16, 16, (4, 4))
     for ref in (va0, wa0, vb0, wb0, va1, wa1, vb1, wb1, kap2, va2, wa2, vb2, wb2, xs2):
         zero(ref)
+    hear(NEXT, news.at[0])
+    tell(OVER, news.at[1])
+    hear(OVER, news.at[1])
+    tell(FLAT, news.at[2])
     x0_arrive()
-
     def put(a):
         def write(p, value):
             ext[a, p, 2] = value
@@ -400,20 +406,17 @@
             w_ref[at] = kap * new
 
     level0 = (kap0, dia0, inv0)
-    start_level(level0, (lo, hi), 4, 16, theta0, lambda at: ext[(0,) + at], res0, va0, wa0, True)
+    start_level(level0, (lo, hi), 4, 16, theta0, lambda at: ext[(0,) + at], res0, va0, wa0, True, FINE)
 
     def own0(ref):
         return ref[P0 : P0 + 8, 0:2, W0 : W0 + 8, :]
 
-    def put_res0(first, n, r):
-        res0[pl.ds(first, n), :, 4:20, :] = r
-
     xs0[...] = own0(va0)
     here, there = (va0, wa0), (vb0, wb0)
 
     def smooth0(step, r_in):
         nonlocal here, there
-        apply(level0, here, r_in, put_res0, (P0 - 3 + step, P0 + 11 - step), 4, 16, weights0[step], there)
+        apply(level0, here, r_in, res0, (P0 - 3 + step, P0 + 11 - step), 4, 16, weights0[step], there, FINE)
         xs0[...] += own0(there[0])
         here, there = there, here
 
@@ -429,29 +432,31 @@
         at = (pl.ds(first, n), slice(None), pl.ds(W1, 8), slice(None))
         value = 128.0 * kap1[at] + stencil_sum(kap1, first, n, W1, 8)
         dia1[first : first + n, :, W1 : W1 + 4, :] = value[:, :, 0:4]
-    d1_arrive, d1_left = exchange(coarse_moves(dia1, 4, True), 32, 32, 0)
+    hear(FLAT, news.at[2])
+    d1_arrive, d1_left = exchange(coarse_moves(dia1, 4, True), 32, 32, None)
+    smooth0(2, lambda at: res0[at])
+
+    def put_rext(first, n, r):
+        rext[0, pl.ds(first, n), 0:2, W0 : W0 + 8, :] = r[:, 0:2]
+
+    apply(level0, here, lambda at: res0[at], put_rext, (P0, P0 + 8), W0, 8, None, None, FINE)
+
+    own_b1 = coarse_of(lambda i, parity, t: rext[0, P0 + i, t, pl.ds(W0 + parity, 4, stride=2), :], 4, 4)
+    for i, value in enumerate(own_b1):
+        bin1[P1 + i, W1 : W1 + 4, :] = value
+    pack_coarse(bedge_out)
+    b1_arrive, b1_left = exchange(edge_moves(bedge_out, bedge_in, W1, 4, 4) + coarse_moves(bin1, 4, False), 16, 16, (4, 4))
     own_k2 = coarse_of(lambda i, parity, t: kap1[P1 + i, t, pl.ds(W1 + parity, 2, stride=2), :], 2, 2)
     for i, value in enumerate(own_k2):
         kin2[P2 + 2 * mx + i, 0, W2 : W2 + 2, :] = 0.25 * value
     k2_arrive, k2_left = column_gather(kin2)
-    smooth0(2, lambda at: res0[at])
-
-    def put_rext(first, n, r):
-        rext[0, pl.ds(first, n), 0:2, W0 : W0 + 8, :] = r[:, 0:2]
-
-    apply(level0, here, lambda at: res0[at], put_rext, (P0, P0 + 8), W0, 8, None)
-
-    own_b1 = coarse_of(lambda i, parity, t: rext[0, P0 + i, t, pl.ds(W0 + parity, 4, stride=2), :], 4, 4)
-    for i, value in enumerate(own_b1):
-        bin1[P1 + i, W1 : W1 + 4, :] = value
-    pack_coarse(bedge_out)
-    b1_arrive, b1_left = exchange(edge_moves(bedge_out, bedge_in, 4) + coarse_moves(bin1, 4, False), 16, 16, 4)
     pack_edges([lambda i, t: rext[0, P0 + i, t, W0 : W0 + 8, :]], redge_out)
     x0_left()
     k1_left()
     d1_arrive()
     d1_left()
     b1_arrive()
+    r0_arrive, r0_left = exchange(edge_moves(redge_out, redge_in, W0, 8, 4) + fine_moves(rext.at[0], 4), 64, 32, (8, 4))
     for p in range(12):
         res1[p, 0] = bin1[p]
         res1[p, 1] = unpack_coarse(bedge_in, p)
@@ -461,13 +466,11 @@
     def own1(ref):
         return ref[P1 : P1 + 4, :, W1 : W1 + 8, :]
 
-    def put_res1(first, n, r):
-        res1[pl.ds(first, n), :, 4:20, :] = r
-
     xs1[...] = own1(va1)
     here, there = (va1, wa1), (vb1, wb1)
     for step in range(3):
-        apply(level1, here, lambda at: res1[at], put_res1, (P1 - 3 + step, P1 + 7 - step), 4, 16, weights0[step], there)
+        at_row, rows = ((4, 16), (6, 8), (7, 8))[step]
+        apply(level1, here, lambda at: res1[at], res1, (P1 - 3 + step, P1 + 7 - step), at_row, rows, weights0[step], there)
         xs1[...] += own1(there[0])
         here, there = there, here
 
@@ -480,9 +483,9 @@
     for i, value in enumerate(own_b2):
         bin2[P2 + 2 * mx + i, 0, W2 : W2 + 2, :] = value
     b2_arrive, b2_left = plane_gather(bin2)
-    r1_arrive, r1_left = exchange(coarse_moves(rex1, 3, True), 24, 18, 0)
     k2_arrive()
     m2_arrive, m2_left = row_gather(kin2)
+    r1_arrive, r1_left = exchange(coarse_moves(rex1, 3, True), 24, 18, None)
     k2_left()
     b1_left()
     m2_arrive()
@@ -495,17 +498,14 @@
     theta2, weights2 = chebyshev_coefs(COARSE_DEGREE, COARSE_LOW)
     level2 = (kap2, dia2, inv2)
     b2_arrive()
-    r0_arrive, r0_left = exchange(edge_moves(redge_out, redge_in, 8) + fine_moves(rext.at[0], 4), 64, 32, 8)
     start_level(level2, (P2, P2 + full), 8, 24, theta2, lambda at: bin2[at], res2, va2, wa2, True)
-    xs2[window] = va2[window]
+    near = (slice(P2, P2 + full), slice(None), slice(W2 - 3, W2 + 5), slice(None))
+    xs2[near] = va2[near]
     here, there = (va2, wa2), (vb2, wb2)
-
-    def put_res2(first, n, r):
-        res2[pl.ds(first, n), :, 8:32, :] = r
-
     for step in range(COARSE_DEGREE - 1):
-        apply(level2, here, lambda at: res2[at], put_res2, (P2, P2 + full), 8, 24, weights2[step], there)
-        xs2[window] += there[0][window]
+        at_row, rows = (8, 24) if step == 0 else ((W2 - 7, 16) if step < 5 else (W2 - 3, 8))
+        apply(level2, here, lambda at: res2[at], res2, (P2, P2 + full), at_row, rows, weights2[step], there)
+        xs2[near] += there[0][near]
         here, there = there, here
 
     half = lanes_of((8, 128)) // 2
@@ -521,15 +521,16 @@
     xs1[...] += own1(va1)
     r1_arrive()
     here, there = (va1, wa1), (vb1, wb1)
-    apply(level1, here, lambda at: rex1[at], put_res1, (P1 - 3, P1 + 7), 4, 16, (None, theta0), there)
+    apply(level1, here, lambda at: rex1[at], res1, (P1 - 3, P1 + 7), 4, 16, (None, theta0), there)
     xs1[...] += own1(there[0])
     here, there = there, here
     for step in range(3):
-        apply(level1, here, lambda at: res1[at], put_res1, (P1 - 2 + step, P1 + 6 - step), 4, 16, weights0[step], there)
+        at_row = (6, 7, 8)[step]
+        apply(level1, here, lambda at: res1[at], res1, (P1 - 2 + step, P1 + 6 - step), at_row, 8, weights0[step], there)
         xs1[...] += own1(there[0])
         here, there = there, here
     xex1[P1 : P1 + 4, :, W1 : W1 + 4, :] = xs1[:, :, 0:4, :]
-    x1_arrive, x1_left = exchange(coarse_moves(xex1, 3, True), 24, 18, 0)
+    x1_arrive, x1_left = exchange(coarse_moves(xex1, 3, True), 24, 18, None)
     b2_left()
     r1_left()
     r0_left()
@@ -554,7 +555,7 @@
         wa0[first : first + n] = kap0[first : first + n] * va0[first : first + n]
     xs0[...] += own0(va0)
     here, there = (va0, wa0), (vb0, wb0)
-    apply(level0, here, lambda at: rext[(0,) + at], put_res0, (lo, hi), 4, 16, (None, theta0), there)
+    apply(level0, here, lambda at: rext[(0,) + at], res0, (lo, hi), 4, 16, (None, theta0), there, FINE)
     xs0[...] += own0(there[0])
     here, there = there, here
     for step in range(3):
@@ -564,7 +565,7 @@
         for tile in range(2):
             r_ref[first - P0 : first - P0 + n, :, 128 * tile : 128 * tile + 128] = r[:, tile]
 
-    apply(level0, here, lambda at: res0[at], put_out, (P0, P0 + 8), W0, 8, None)
+    apply(level0, here, lambda at: res0[at], put_out, (P0, P0 + 8), W0, 8, None, None, FINE)
     for tile in range(2):
         x_ref[:, :, 128 * tile : 128 * tile + 128] = xs0[:, tile]
     x1_left()
@@ -593,6 +594,7 @@
                 *[vmem(*level2) for _ in range(11)],
                 vmem(2, 16, 128), vmem(24, 128), vmem(1152, 128),
                 pltpu.SemaphoreType.DMA((sems,)), pltpu.SemaphoreType.DMA((sems,)), pltpu.SemaphoreType.DMA((4,)),
+                pltpu.SemaphoreType.REGULAR((3,)),
             ],
             compiler_params=pltpu.CompilerParams(
                 collective_id=0, has_side_effects=True, vmem_limit_bytes=50 * 1024 * 1024

time: 48.3 us -> 44.8 us (0.928)
  Pallas kernels: 46.2 us -> 42.7 us
    pallas_call x1, Pallas kernels: 46.2 us -> 42.7 us  [step(): pl.pallas_call(lambda *refs: kernel(sizes, *refs), name='cycle', out_shap...]
where the time goes in v2:
time: 44.8 us; the launch traced here: 44.6 us
  Pallas kernels  42.7 us (95%)
  local copies, waits for them, and re-layouts  1.26 us (3%)
  between operations  0.64 us (1%)
    pallas_call x1, Pallas kernels, step(): pl.pallas_call(lambda *refs: kernel(sizes, *refs), name='cycle', out_shap...  42.7 us
    unnamed x2, local copies, waits for them, and re-layouts  1.26 us

profile of v2, /device:TPU:1, one launch (start us, length us, event | category | flops | bytes accessed | tf_op | source)
XLA Modules:
  0.0 44.6 jit_solution(9041221683066453729)
XLA Ops:
  0.6 42.7 %cycle.1 = (f32[8,8,256]{2,1,0:T(8,128)S(1)}, f32[8,8,256]{2,1,0:T(8,128)S(1)}) custom-call(f32[8,8,256]{2,1,0:T(8,128)} %refs_0_.1, f32[8,8,256]{2,1,0:T(8,128)} %refs_1_.1), custom_call_target="tpu_custom_call" | custom-call | tf_op jit(solution)/shard_map/cycle/pallas_call | solution.py:584
  43.3 0.6 %copy.6 = f32[8,8,256]{2,1,0:T(8,128)} copy(f32[8,8,256]{2,1,0:T(8,128)S(1)} %get-tuple-element.4) | data formatting | bytes 131072
  44.0 0.6 %copy.7 = f32[8,8,256]{2,1,0:T(8,128)} copy(f32[8,8,256]{2,1,0:T(8,128)S(1)} %get-tuple-element.5) | data formatting | bytes 131072

commit v3 on v2

--- a/solution.py
+++ b/solution.py
@@ -176,12 +176,11 @@
                     cases.append((where, (x + y) * face + x * y * corner + (z * (1 + x) * (stack[0] + y * stack[1]) if stack else 0)))
         return waits(number, cases)
 
-    def mine(ref):
-        return ref.at[pl.ds(P2 + 2 * mx, 2), :, pl.ds(W2, 2), :]
-
-    def far_start(ref, number, shift, j):
+    def far_start(ref, number, shift, j, thin=False):
+        first, rows = (W2 + (1 if j > 0 else 0), 1) if thin else (W2, 2)
+        planes = pl.ds(P2 + 2 * mx, 2)
         copy = pltpu.make_async_remote_copy(
-            src_ref=mine(ref), dst_ref=ref.at[pl.ds(P2 + 2 * mx, 2), :, pl.ds(W2 - 2 * j, 2), :],
+            src_ref=ref.at[planes, :, pl.ds(first, rows), :], dst_ref=ref.at[planes, :, pl.ds(first - 2 * j, rows), :],
             send_sem=send.at[number], recv_sem=recv.at[number],
             device_id=(lax.rem(mx + shift, nx), my + j, mz), device_id_type=MESH,
         )
@@ -206,8 +205,13 @@
         for j in distances:
             for shift in range(nx):
                 if (shift, j) != (0, 0):
-                    far_start(ref, number, shift, j)
-        return waits(number, [(low_y + high_y == c, 4 * ((1 + c) * nx - 1)) for c in far_counts])
+                    far_start(ref, number, shift, j, abs(j) == REACH)
+        cases = {}
+        for y in range(ny):
+            c = min(y, REACH) + min(ny - 1 - y, REACH)
+            thin = (y >= REACH) + (y + REACH < ny)
+            assert cases.setdefault(c, thin) == thin
+        return waits(number, [(low_y + high_y == c, 4 * ((1 + c) * nx - 1) - 2 * thin * nx) for c, thin in cases.items()])
 
     def row_gather(ref):
         number = used[0]
@@ -331,17 +335,22 @@
         with jax.named_scope("hear"):
             pl.semaphore_wait(semaphore, sum(jnp.where(inside(i, j, k), 1, 0) for i, j, k in offsets))
 
-    tell(STACK + FLAT, barrier)
+    for i, j, k in STACK + FLAT:
+        ok = inside(i, j, k)
+        to = tuple(jnp.where(ok, m + step, m) for m, step in ((mx, i), (my, j), (mz, k)))
+        pl.semaphore_signal(barrier, inc=1, device_id=to, device_id_type=MESH)
     zero(tmp)
     zero(tmp2)
     for copy in loads:
         copy.wait()
     pack_edges([lambda i, t: ext[0, P0 + i, t, W0 : W0 + 8, :], lambda i, t: ext[1, P0 + i, t, W0 : W0 + 8, :]], edge_out)
-    hear(STACK + FLAT, barrier)
-    moves = edge_moves(edge_out, edge_in, W0, 8, 5)
+    with jax.named_scope("barrier"):
+        pl.semaphore_wait(barrier, 26)
+    edges_arrive, edges_left = exchange(edge_moves(edge_out, edge_in, W0, 8, 5), 0, 0, (8, 5))
+    moves = []
     for (offset, src_b, dst_b), (_, src_k, dst_k) in zip(fine_moves(ext.at[0], 4), fine_moves(ext.at[1], 5)):
         moves += [(offset, src_b, dst_b), (offset, src_k, dst_k)]
-    x0_arrive, x0_left = exchange(moves, 144, 82, (8, 5))
+    x0_arrive, x0_left = exchange(moves, 144, 82, None)
 
     tell(NEXT, news.at[0])
 
@@ -358,7 +367,8 @@
     tell(OVER, news.at[1])
     hear(OVER, news.at[1])
     tell(FLAT, news.at[2])
-    x0_arrive()
+    edges_arrive()
+
     def put(a):
         def write(p, value):
             ext[a, p, 2] = value
@@ -367,6 +377,7 @@
 
     unpack_edges(edge_in, 0, put(0))
     unpack_edges(edge_in, 1, put(1))
+    x0_arrive()
     row = lax.broadcasted_iota(jnp.int32, (24, 128), 0)
 
     def planes_in(p, own, width):
@@ -451,12 +462,12 @@
         kin2[P2 + 2 * mx + i, 0, W2 : W2 + 2, :] = 0.25 * value
     k2_arrive, k2_left = column_gather(kin2)
     pack_edges([lambda i, t: rext[0, P0 + i, t, W0 : W0 + 8, :]], redge_out)
+    edges_left()
     x0_left()
     k1_left()
     d1_arrive()
     d1_left()
     b1_arrive()
-    r0_arrive, r0_left = exchange(edge_moves(redge_out, redge_in, W0, 8, 4) + fine_moves(rext.at[0], 4), 64, 32, (8, 4))
     for p in range(12):
         res1[p, 0] = bin1[p]
         res1[p, 1] = unpack_coarse(bedge_in, p)
@@ -486,6 +497,7 @@
     k2_arrive()
     m2_arrive, m2_left = row_gather(kin2)
     r1_arrive, r1_left = exchange(coarse_moves(rex1, 3, True), 24, 18, None)
+    r0_arrive, r0_left = exchange(edge_moves(redge_out, redge_in, W0, 8, 4) + fine_moves(rext.at[0], 4), 64, 32, (8, 4))
     k2_left()
     b1_left()
     m2_arrive()
@@ -579,7 +591,7 @@
             return pltpu.VMEM(shape, F32)
 
         level0, level1, level2 = (18, 3, 24, 128), (12, 2, 24, 128), (12, 1, 40, 128)
-        sems = 10
+        sems = 11
         shape = jax.ShapeDtypeStruct(conductivity.shape, F32)
         return pl.pallas_call(
             lambda *refs: kernel(sizes, *refs),

time: 44.8 us -> 43.9 us (0.980)
  Pallas kernels: 42.7 us -> 41.6 us
    pallas_call x1, Pallas kernels: 42.7 us -> 41.6 us  [step(): pl.pallas_call(lambda *refs: kernel(sizes, *refs), name='cycle', out_shap...]
where the time goes in v3:
time: 43.9 us; the launch traced here: 43.5 us
  Pallas kernels  41.6 us (95%)
  local copies, waits for them, and re-layouts  1.26 us (3%)
  between operations  0.64 us (1%)
    pallas_call x1, Pallas kernels, step(): pl.pallas_call(lambda *refs: kernel(sizes, *refs), name='cycle', out_shap...  41.6 us
    unnamed x2, local copies, waits for them, and re-layouts  1.26 us

profile of v3, /device:TPU:1, one launch (start us, length us, event | category | flops | bytes accessed | tf_op | source)
XLA Modules:
  0.0 43.5 jit_solution(11646711971555567195)
XLA Ops:
  0.6 41.6 %cycle.1 = (f32[8,8,256]{2,1,0:T(8,128)S(1)}, f32[8,8,256]{2,1,0:T(8,128)S(1)}) custom-call(f32[8,8,256]{2,1,0:T(8,128)} %refs_0_.1, f32[8,8,256]{2,1,0:T(8,128)} %refs_1_.1), custom_call_target="tpu_custom_call" | custom-call | tf_op jit(solution)/shard_map/cycle/pallas_call | solution.py:596
  42.2 0.6 %copy.6 = f32[8,8,256]{2,1,0:T(8,128)} copy(f32[8,8,256]{2,1,0:T(8,128)S(1)} %get-tuple-element.4) | data formatting | bytes 131072
  42.9 0.6 %copy.7 = f32[8,8,256]{2,1,0:T(8,128)} copy(f32[8,8,256]{2,1,0:T(8,128)S(1)} %get-tuple-element.5) | data formatting | bytes 131072

commit v4 on v3

--- a/solution.py
+++ b/solution.py
@@ -206,12 +206,12 @@
             for shift in range(nx):
                 if (shift, j) != (0, 0):
                     far_start(ref, number, shift, j, abs(j) == REACH)
-        cases = {}
-        for y in range(ny):
-            c = min(y, REACH) + min(ny - 1 - y, REACH)
-            thin = (y >= REACH) + (y + REACH < ny)
-            assert cases.setdefault(c, thin) == thin
-        return waits(number, [(low_y + high_y == c, 4 * ((1 + c) * nx - 1) - 2 * thin * nx) for c, thin in cases.items()])
+        thin_y = jnp.where(my >= REACH, 1, 0) + jnp.where(my + REACH < ny, 1, 0)
+        cases = sorted({(min(y, REACH) + min(ny - 1 - y, REACH), (y >= REACH) + (y + REACH < ny)) for y in range(ny)})
+        return waits(
+            number,
+            [((low_y + high_y == c) & (thin_y == t), 4 * ((1 + c) * nx - 1) - 2 * t * nx) for c, t in cases],
+        )
 
     def row_gather(ref):
         number = used[0]
@@ -601,10 +601,10 @@
             out_specs=(pl.BlockSpec(memory_space=pltpu.VMEM),) * 2,
             scratch_shapes=[
                 vmem(2, *level0), vmem(2, 3, 24, 128), vmem(2, 8, 128), vmem(2, 3, 24, 128), vmem(2, 8, 128), vmem(1, *level0),
-                *[vmem(*level0) for _ in range(8)], vmem(8, 2, 8, 128),
+                *[vmem(*level0) for _ in range(4)], vmem(19, 3, 24, 128), *[vmem(*level0) for _ in range(3)], vmem(8, 2, 8, 128),
                 vmem(12, 24, 128), vmem(12, 24, 128), *[vmem(*s) for s in 2 * ((2, 3, 24, 128), (2, 8, 128))], *[vmem(*level1) for _ in range(10)], vmem(4, 2, 8, 128),
                 *[vmem(*level2) for _ in range(11)],
-                vmem(2, 16, 128), vmem(24, 128), vmem(1152, 128),
+                vmem(2, 24, 128), vmem(24, 128), vmem(1152, 128),
                 pltpu.SemaphoreType.DMA((sems,)), pltpu.SemaphoreType.DMA((sems,)), pltpu.SemaphoreType.DMA((4,)),
                 pltpu.SemaphoreType.REGULAR((3,)),
             ],

time: 43.9 us -> 43.9 us (level)
  no operation moved by 1% of the time
where the time goes in v4:
time: 43.9 us; the launch traced here: 43.5 us
  Pallas kernels  41.6 us (95%)
  local copies, waits for them, and re-layouts  1.26 us (3%)
  between operations  0.64 us (1%)
    pallas_call x1, Pallas kernels, step(): pl.pallas_call(lambda *refs: kernel(sizes, *refs), name='cycle', out_shap...  41.6 us
    unnamed x2, local copies, waits for them, and re-layouts  1.26 us

profile of v4, /device:TPU:1, one launch (start us, length us, event | category | flops | bytes accessed | tf_op | source)
XLA Modules:
  0.0 43.5 jit_solution(1964644259002354778)
XLA Ops:
  0.6 41.6 %cycle.1 = (f32[8,8,256]{2,1,0:T(8,128)S(1)}, f32[8,8,256]{2,1,0:T(8,128)S(1)}) custom-call(f32[8,8,256]{2,1,0:T(8,128)} %refs_0_.1, f32[8,8,256]{2,1,0:T(8,128)} %refs_1_.1), custom_call_target="tpu_custom_call" | custom-call | tf_op jit(solution)/shard_map/cycle/pallas_call | solution.py:596
  42.2 0.6 %copy.6 = f32[8,8,256]{2,1,0:T(8,128)} copy(f32[8,8,256]{2,1,0:T(8,128)S(1)} %get-tuple-element.4) | data formatting | bytes 131072
  42.9 0.6 %copy.7 = f32[8,8,256]{2,1,0:T(8,128)} copy(f32[8,8,256]{2,1,0:T(8,128)S(1)} %get-tuple-element.5) | data formatting | bytes 131072

commit v5 on v4

--- a/solution.py
+++ b/solution.py
@@ -74,7 +74,7 @@
     return [(at, min(size, last - at)) for at in range(first, last, size)]
 
 
-def apply(level, source, r_in, r_out, planes, row, rows, coefs, target=None, size=2):
+def apply(level, source, r_in, r_out, planes, row, rows, coefs, target=None, size=3):
     kappa, diagonal, inverse = level
     v_ref, w_ref = source
     for first, count in chunks(planes[0], planes[1], size):
@@ -398,7 +398,7 @@
     theta0, weights0 = chebyshev_coefs(DEGREE, FINE_LOW)
     lo, hi = P0 - 4, P0 + 12
 
-    def start_level(level, planes, row, rows, theta, r_in, r_out, v_ref, w_ref, make_diagonal, size=2):
+    def start_level(level, planes, row, rows, theta, r_in, r_out, v_ref, w_ref, make_diagonal, size=3):
         kappa, diagonal, inverse = level
         for first, n in chunks(planes[0], planes[1], size):
             at = (pl.ds(first, n), slice(None), pl.ds(row, rows), slice(None))
@@ -510,13 +510,13 @@
     theta2, weights2 = chebyshev_coefs(COARSE_DEGREE, COARSE_LOW)
     level2 = (kap2, dia2, inv2)
     b2_arrive()
-    start_level(level2, (P2, P2 + full), 8, 24, theta2, lambda at: bin2[at], res2, va2, wa2, True)
+    start_level(level2, (P2, P2 + full), 8, 24, theta2, lambda at: bin2[at], res2, va2, wa2, True, 1)
     near = (slice(P2, P2 + full), slice(None), slice(W2 - 3, W2 + 5), slice(None))
     xs2[near] = va2[near]
     here, there = (va2, wa2), (vb2, wb2)
     for step in range(COARSE_DEGREE - 1):
         at_row, rows = (8, 24) if step == 0 else ((W2 - 7, 16) if step < 5 else (W2 - 3, 8))
-        apply(level2, here, lambda at: res2[at], res2, (P2, P2 + full), at_row, rows, weights2[step], there)
+        apply(level2, here, lambda at: res2[at], res2, (P2, P2 + full), at_row, rows, weights2[step], there, 1)
         xs2[near] += there[0][near]
         here, there = there, here
 

time: 43.9 us -> 43.9 us (level)
  no operation moved by 1% of the time
where the time goes in v5:
time: 43.9 us; the launch traced here: 43.5 us
  Pallas kernels  41.6 us (95%)
  local copies, waits for them, and re-layouts  1.26 us (3%)
  between operations  0.64 us (1%)
    pallas_call x1, Pallas kernels, step(): pl.pallas_call(lambda *refs: kernel(sizes, *refs), name='cycle', out_shap...  41.6 us
    unnamed x2, local copies, waits for them, and re-layouts  1.26 us

profile of v5, /device:TPU:1, one launch (start us, length us, event | category | flops | bytes accessed | tf_op | source)
XLA Modules:
  0.0 43.5 jit_solution(9947554257684846397)
XLA Ops:
  0.6 41.6 %cycle.1 = (f32[8,8,256]{2,1,0:T(8,128)S(1)}, f32[8,8,256]{2,1,0:T(8,128)S(1)}) custom-call(f32[8,8,256]{2,1,0:T(8,128)} %refs_0_.1, f32[8,8,256]{2,1,0:T(8,128)} %refs_1_.1), custom_call_target="tpu_custom_call" | custom-call | tf_op jit(solution)/shard_map/cycle/pallas_call | solution.py:596
  42.2 0.6 %copy.6 = f32[8,8,256]{2,1,0:T(8,128)} copy(f32[8,8,256]{2,1,0:T(8,128)S(1)} %get-tuple-element.4) | data formatting | bytes 131072
  42.9 0.6 %copy.7 = f32[8,8,256]{2,1,0:T(8,128)} copy(f32[8,8,256]{2,1,0:T(8,128)S(1)} %get-tuple-element.5) | data formatting | bytes 131072
